TPU v7x, 32 devices: a whole 2x2x4 slice. The times are simulated.
32 devices in a mesh: dp: 4 (over x, y), sp: 8 (over z, core).
Axes of the slice: x: 2, y: 2, z: 4, core: 2. Of those that a mesh axis runs over, the one named last changes fastest.
Arguments:
- q: bfloat16 [128, 48, 128], P('dp'), parts along dimension 0
- k: bfloat16 [128, 8192, 8, 128], P('dp', 'sp'), parts along dimension 0
- v: bfloat16 [128, 8192, 8, 128], P('dp', 'sp'), parts along dimension 0
Outputs:
- q: bfloat16 [128, 48, 128], P('dp'), parts along dimension 0
There are 4 independent parts. A program takes and returns all parts, laid end to end along the dimension named above; each array names one.
All inputs are finite; a program needn't handle non-finite values.
Results may differ from a plain program's by a relative error of at most 0.012.
Values are sent between devices in bfloat16 or wider.
A program may use at most 2 GiB of HBM per device.

v0:
```python
import jax
import jax.numpy as jnp
from jax import lax
from jax.sharding import PartitionSpec as P


def einsum(form, a, b):
    return jnp.einsum(form, a.astype(jnp.float32), b.astype(jnp.float32))


def part_of(q, k, v):
    grouped = q.reshape(q.shape[0], k.shape[2], -1, q.shape[2])
    scores = einsum("bgsd,bugd->bgsu", grouped, k) * q.shape[2] ** -0.5
    high = jnp.max(scores, -1, keepdims=True)
    weights = jnp.exp(scores - high)
    seen = einsum("bgsu,bugd->bgsd", weights.astype(jnp.bfloat16), v)
    return jnp.concatenate([seen, jnp.sum(weights, -1, keepdims=True), high], -1)


def together(parts):
    seen, total, high = parts[..., :-2], parts[..., -2:-1], parts[..., -1:]
    scale = jnp.exp(high - jnp.max(high, 0))
    return (jnp.sum(seen * scale, 0) / jnp.sum(total * scale, 0)).astype(jnp.bfloat16)


def solution(mesh):
    def step(q, k, v):
        return together(lax.all_gather(part_of(q, k, v), "sp")).reshape(q.shape)

    return jax.shard_map(
        step,
        mesh=mesh,
        in_specs=(P("dp", None, None), P("dp", "sp", None, None), P("dp", "sp", None, None)),
        out_specs=P("dp", None, None),
        check_vma=False,
    )
```

profile of v0, /device:TPU:0, one launch (start us, length us, event | category | flops | bytes accessed | tf_op | source)
XLA Modules:
  0.0 230.8 jit_solution(7114843656571764980)
XLA Ops:
  6.5 0.0 all-gather.3.cloned.1.call-start
  6.5 1.1 copy.46
  7.6 28.9 %multiply_reduce_fusion = (f32[32,8,6]{2,1,0:T(8,128)S(1)}, f32[32,8,6,1024]{3,2,1,0:T(8,128)}) fusion(bf16[32,1024,8,128]{3,2,1,0:T(8,128)(2,1)} %param.4, bf16[32,8,6,128]{3,0,2,1:T(8,128)(2,1)S(1)} %bitcast.15), kind=kOutput, calls=%fused_computation.5 | convolution fusion | flops 405797376 | bytes 73799680 | tf_op jit(solution)/shard_map/bgsd,bugd->bgsu/dot_general | solution.py:8
  36.6 4.5 %fusion.4 = f32[32,8,6]{2,1,0:T(8,128)S(1)} fusion(f32[32,8,6,1024]{3,2,1,0:T(8,128)} %get-tuple-element.11, f32[32,8,6]{2,1,0:T(8,128)S(1)} %get-tuple-element.10), kind=kLoop, calls=%fused_computation.6 | loop fusion | flops 4717056 | bytes 6303744 | tf_op jit(solution)/shard_map/reduce_sum | solution.py:17
  41.0 30.4 %fusion = f32[32,8,6,128]{3,2,1,0:T(8,128)S(1)} fusion(bf16[32,1024,8,128]{3,2,1,0:T(8,128)(2,1)} %param.5, f32[32,8,6,1024]{3,2,1,0:T(8,128)} %get-tuple-element.11, f32[32,8,6]{2,1,0:T(8,128)S(1)} %get-tuple-element.10), kind=kOutput, calls=%fused_computation | convolution fusion | flops 407371776 | bytes 74192896 | tf_op jit(solution)/shard_map/bgsu,bugd->bgsd/dot_general | solution.py:8
  71.4 1.7 copy.52
  73.1 1.7 copy.53
  74.7 0.4 pad_maximum_fusion
  75.1 1.9 copy.54
  77.0 0.0 all-gather.3.cloned.1.call-update
  77.0 119.2 %all-gather.3.cloned.1.call-done = f32[256,8,6,130]{3,1,2,0:T(8,128)} async-done(((f32[32,8,6,130]{3,1,2,0:T(8,128)}), f32[256,8,6,130]{3,1,2,0:T(8,128)}) %all-gather.3.cloned.1.call-update) | async-done | bytes 6389776 | tf_op jit(solution)/shard_map/all_gather | solution.py:28
  196.2 11.4 %fusion.14 = (f32[8,32,8,6,1]{4,2,3,1,0:T(8,128)}, f32[32,8,6]{1,2,0:T(8,128)S(1)}, f32[8,32,8,6,1]{4,2,3,1,0:T(8,128)}) fusion(f32[8,32,8,6,130]{4,2,3,1,0:T(8,128)} %bitcast.12), kind=kLoop, calls=%fused_computation.21 | loop fusion | flops 10752 | bytes 202752 | tf_op jit(solution)/shard_map/slice | solution.py:21
  207.6 4.9 %copy.68 = f32[8,32,8,6,1]{1,2,4,3,0:T(8,128)S(1)} copy(f32[8,32,8,6,1]{4,2,3,1,0:T(8,128)} %get-tuple-element.5) | data formatting | bytes 98304
  212.5 0.1 copy.70
  212.6 4.9 %copy.67 = f32[8,32,8,6,1]{1,2,4,3,0:T(8,128)S(1)} copy(f32[8,32,8,6,1]{4,2,3,1,0:T(8,128)} %get-tuple-element.7) | data formatting | bytes 98304
  217.6 0.4 copy.56
  218.0 4.5 %fusion.6 = f32[32,8,6,128]{3,1,2,0:T(8,128)S(1)} fusion(f32[8,32,8,6,130]{4,2,3,1,0:T(8,128)} %bitcast.13, f32[8,32,8,6]{2,3,1,0:T(8,128)S(1)} %copy.56), kind=kLoop, calls=%fused_computation.9 | loop fusion | flops 2949120 | bytes 7127040 | tf_op jit(solution)/shard_map/reduce_sum | solution.py:23
  222.5 0.3 copy.58
  222.8 0.3 fusion.10
  223.1 0.9 copy.61
  (3 shorter events, 0.1 us)
Async XLA Ops:
  6.5 189.7 %all-gather.3.cloned.1.call-start = ((), (), s32[]{:S(2)}) async-start(), calls=%async_computation | async-start | bytes 14155776 | tf_op jit(solution)/shard_map/all_gather | solution.py:28
Sparse Core Ops, SparseCore 0:
  77.1 118.9 all-gather.2
where the time goes:
time: 231 us
  waiting for transfers between devices  119 us (52%)
  matrix products  59.3 us (26%)
  other arithmetic  21.1 us (9%)
  local copies, waits for them, and re-layouts  17.8 us (8%)
  between operations  13.5 us (6%)
    all_gather x1, waiting for transfers between devices, step(): return together(lax.all_gather(part_of(q, k, v), 'sp')).reshape(q.shape)  119 us
    dot_general x2, matrix products, einsum(): return jnp.einsum(form, a.astype(jnp.float32), b.astype(jnp.float32))  59.3 us
    slice x1, other arithmetic, together(): seen, total, high = (parts[..., :-2], parts[..., -2:-1], parts[..., -1:])  11.4 us
    unnamed x4, local copies, waits for them, and re-layouts  11 us
  transfers between devices with their start and end apart: 1, of which 1 were waited for; matrix products, arithmetic and copies ran while one was open for 0% of the time, Pallas kernels for 0%

commit v1 on v0

v1 whole, which is shorter than its diff:
```python
import functools
import math

import jax
import jax.numpy as jnp
from jax import lax
from jax.experimental import pallas as pl
from jax.experimental.pallas import tpu as pltpu
from jax.sharding import PartitionSpec as P

F32, BF16 = jnp.float32, jnp.bfloat16
RING = 6
LAG = 6
DIRECT = 2
TILE = 256


def kernel(group, q_ref, k_hbm, v_hbm, out_hbm, kbuf, vbuf, s0, s1, m0, m1, parts, stats, res, ksem, vsem, osem,
           po_send, ps_send, po_recv, ps_recv, r_send, r_recv):
    n, rows, d = k_hbm.shape
    heads = q_ref.shape[1]
    kv_heads = 8
    half = rows // 2
    tiles = half // TILE
    c = d**-0.5 * math.log2(math.e)
    me = lax.axis_index("sp")
    owned = n - DIRECT
    full = owned // group
    tail = full * group

    def kcopy(i):
        return pltpu.make_async_copy(k_hbm.at[i], kbuf.at[lax.rem(i, RING)], ksem.at[lax.rem(i, RING)])

    def vcopy(i):
        return pltpu.make_async_copy(v_hbm.at[i], vbuf.at[lax.rem(i, RING)], vsem.at[lax.rem(i, RING)])

    kcopy(0).start()
    for i in range(1, RING):
        kcopy(i).start()
        vcopy(i - 1).start()
    vcopy(RING - 1).start()

    barrier = pltpu.get_barrier_semaphore()
    for step in range(1, group):
        pl.semaphore_signal(barrier, inc=1, device_id={"sp": lax.rem(me + step, group)}, device_id_type=pl.DeviceIdType.MESH)

    shape = (heads, TILE)
    own_head = lax.broadcasted_iota(jnp.int32, shape, 0) // (heads // kv_heads) == lax.broadcasted_iota(jnp.int32, shape, 1) % kv_heads
    mask = jnp.concatenate([own_head, own_head], 0)
    row = lax.broadcasted_iota(jnp.int32, (heads, d), 0)
    lane = lax.broadcasted_iota(jnp.int32, (heads, d), 1)

    def side(ref, slot, t):
        return jnp.concatenate([ref[slot, t * TILE : (t + 1) * TILE, :], ref[slot, half + t * TILE : half + (t + 1) * TILE, :]], 1)

    def scores(i, s_ref, m_ref):
        slot = lax.rem(i, RING)
        q = q_ref[i]
        z = jnp.zeros_like(q)
        qq = jnp.concatenate([jnp.concatenate([q, z], 1), jnp.concatenate([z, q], 1)], 0)
        m = jnp.full((2 * heads, d), -jnp.inf, F32)
        for t in range(tiles):
            s = lax.dot_general(qq, side(kbuf, slot, t), (((1,), (1,)), ((), ())), preferred_element_type=F32)
            s = jnp.where(mask, s, -jnp.inf)
            s_ref[:, t * TILE : (t + 1) * TILE] = s
            m = jnp.maximum(m, jnp.maximum(s[:, :d], s[:, d:]))
        m_ref[...] = m

    def attend(i, s_ref, m_ref):
        slot = lax.rem(i, RING)
        m = m_ref[...]
        m = jnp.max(jnp.maximum(m[:heads], m[heads:]), 1, keepdims=True)
        m2 = jnp.concatenate([m, m], 0)
        l = jnp.zeros((2 * heads, d), F32)
        o = jnp.zeros((2 * heads, TILE), F32)
        for t in range(tiles):
            p = jnp.exp2((s_ref[:, t * TILE : (t + 1) * TILE] - m2) * c)
            l = l + (p[:, :d] + p[:, d:])
            o = o + lax.dot_general(p.astype(BF16), side(vbuf, slot, t), (((1,), (0,)), ((), ())), preferred_element_type=F32)
        l = jnp.sum(l[:heads] + l[heads:], 1, keepdims=True)
        parts[i, me] = (o[:heads, :d] + o[heads:, d:]).astype(BF16)
        stats[i, me] = jnp.sum(jnp.where(lane == row, m, jnp.where(lane == row + d // 2, l, 0.0)), 0, keepdims=True)

    def owner(i):
        return lax.rem(i + 2 * group - owned % group + 4, group)

    def index(i):
        if isinstance(i, int):
            return i // group if i < tail else full + i - tail
        return jnp.where(i < tail, i // group, full + i - tail)

    def part_copies(i, to):
        at = index(i)
        return [
            pltpu.make_async_remote_copy(ref.at[i, me], ref.at[i, me], send.at[at], recv.at[at], device_id={"sp": to}, device_id_type=pl.DeviceIdType.MESH)
            for ref, send, recv in ((parts, po_send, po_recv), (stats, ps_send, ps_recv))
        ]

    def result_copy(i, to):
        return pltpu.make_async_remote_copy(res.at[i], res.at[i], r_send.at[index(i)], r_recv.at[index(i)], device_id={"sp": to}, device_id_type=pl.DeviceIdType.MESH)

    def wait(ref, sem):
        pltpu.make_async_copy(ref, ref, sem).wait()

    def send_part(i):
        @pl.when(me != owner(i))
        def _():
            for copy in part_copies(i, owner(i)):
                copy.start()

    def send_all(copy_to):
        for step in range(1, group):
            copy_to(lax.rem(me + step, group))

    def wait_parts(i):
        wait(parts.at[i, : group - 1], po_recv.at[index(i)])
        wait(stats.at[i, : group - 1], ps_recv.at[index(i)])

    def together(i):
        st = stats[i, :, 0, :]
        w = jnp.exp2((st - jnp.max(st, 0, keepdims=True)) * c)
        w = w / jnp.sum(w * pltpu.roll(st, d // 2, 1), 0, keepdims=True)
        w = jnp.transpose(w)
        out = w[:heads, :1] * parts[i, 0].astype(F32)
        for s in range(1, group):
            out = out + w[:heads, s : s + 1] * parts[i, s].astype(F32)
        res[i] = out.astype(BF16)

    def owner_step(i):
        @pl.when(me == owner(i))
        def _():
            wait_parts(i)
            together(i)

    def owner_send(i):
        @pl.when(me == owner(i))
        def _():
            send_all(lambda to: result_copy(i, to).start())

    def exchange(i, back):
        if isinstance(i, int):
            if i >= back:
                return lambda f: f(i - back)
            return lambda f: None
        return lambda f: pl.when(i >= back)(lambda: f(i - back))

    def half_step(i, sa, ma, sb, mb):
        if not isinstance(i, int) or i + 1 < n:
            kcopy(i + 1).wait()
        vcopy(i).wait()
        if not isinstance(i, int) or i + 1 < n:
            scores(i + 1, sb, mb)
        attend(i, sa, ma)
        if not isinstance(i, int):
            @pl.when(i + 1 + RING < n)
            def _():
                kcopy(i + 1 + RING).start()

            @pl.when(i + RING < n)
            def _():
                vcopy(i + RING).start()
            send_part(i)
        else:
            for step in range(group - 1, 0, -1):
                for copy in part_copies(i, lax.rem(me + step, group)):
                    copy.start()
        exchange(i, LAG + 1)(owner_send)
        exchange(i, LAG)(owner_step)

    kcopy(0).wait()
    scores(0, s0, m0)
    kcopy(RING).start()
    pl.semaphore_wait(barrier, group - 1)

    def body(j, _):
        half_step(2 * j, s0, m0, s1, m1)
        half_step(2 * j + 1, s1, m1, s0, m0)
        return 0

    lax.fori_loop(0, owned // 2, body, 0)
    for i in range(owned, n):
        a, b = ((s0, m0), (s1, m1)) if i % 2 == 0 else ((s1, m1), (s0, m0))
        half_step(i, *a, *b)

    owner_send(n - 1 - LAG)
    for i in range(n - LAG, owned):
        owner_step(i)
        owner_send(i)
    for i in range(owned, n):
        wait_parts(i)
        together(i)

    for b in range(full):
        wait(res.at[: group - 1], r_recv.at[b])
    for i in range(tail, owned):
        @pl.when(me != owner(i))
        def _():
            wait(res.at[i], r_recv.at[index(i)])
    out = pltpu.make_async_copy(res, out_hbm, osem)
    out.start()

    for b in range(full):
        wait(parts.at[0, : group - 1], po_send.at[b])
        wait(stats.at[0, : group - 1], ps_send.at[b])
        wait(res.at[: group - 1], r_send.at[b])
    for i in range(tail, owned):
        @pl.when(me != owner(i))
        def _():
            wait(parts.at[i, 0], po_send.at[index(i)])
            wait(stats.at[i, 0], ps_send.at[index(i)])

        @pl.when(me == owner(i))
        def _():
            wait(res.at[: group - 1], r_send.at[index(i)])
    for i in range(owned, n):
        wait(parts.at[i, : group - 1], po_send.at[index(i)])
        wait(stats.at[i, : group - 1], ps_send.at[index(i)])
    out.wait()


def attention(group, q, k, v):
    n, heads, d = q.shape
    rows = k.shape[1] * k.shape[2]
    k, v = k.reshape(n, rows, d), v.reshape(n, rows, d)
    full = (n - DIRECT) // group
    sems = full + n - full * group
    anywhere = pl.BlockSpec(memory_space=pl.ANY)
    return pl.pallas_call(
        functools.partial(kernel, group),
        out_shape=jax.ShapeDtypeStruct((n, heads, d), BF16),
        in_specs=[pl.BlockSpec(memory_space=pltpu.VMEM), anywhere, anywhere],
        out_specs=anywhere,
        scratch_shapes=[
            pltpu.VMEM((RING, rows, d), BF16),
            pltpu.VMEM((RING, rows, d), BF16),
            pltpu.VMEM((2 * heads, rows // 2), F32),
            pltpu.VMEM((2 * heads, rows // 2), F32),
            pltpu.VMEM((2 * heads, d), F32),
            pltpu.VMEM((2 * heads, d), F32),
            pltpu.VMEM((n, group, heads, d), BF16),
            pltpu.VMEM((n, group, 1, d), F32),
            pltpu.VMEM((n, heads, d), BF16),
            pltpu.SemaphoreType.DMA((RING,)),
            pltpu.SemaphoreType.DMA((RING,)),
            pltpu.SemaphoreType.DMA,
        ]
        + [pltpu.SemaphoreType.DMA((sems,))] * 6,
        compiler_params=pltpu.CompilerParams(collective_id=0, has_side_effects=True, vmem_limit_bytes=48 * 2**20),
        cost_estimate=pl.CostEstimate(flops=8 * n * heads * rows * d, bytes_accessed=4 * n * rows * d, transcendentals=n * heads * rows),
    )(q, k, v)


def solution(mesh):
    cache = P("dp", "sp", None, None)
    return jax.shard_map(
        functools.partial(attention, mesh.shape["sp"]),
        mesh=mesh,
        in_specs=(P("dp", None, None), cache, cache),
        out_specs=P("dp", None, None),
        check_vma=False,
    )
```

time: 231 us -> 58.1 us (0.25)
  waiting for transfers between devices: 119 us -> 0 us
  matrix products: 59.3 us -> 0 us
  Pallas kernels: 0 us -> 56.2 us
  other arithmetic: 21.1 us -> 0 us
  local copies, waits for them, and re-layouts: 17.8 us -> 1.74 us
  between operations: 13.5 us -> 0.01 us
    all_gather x1 -> x0, waiting for transfers between devices: 119 us -> none  [step(): return together(lax.all_gather(part_of(q, k, v), 'sp')).reshape(q.shape)]
    dot_general x2 -> x0, matrix products: 59.3 us -> none  [einsum(): return jnp.einsum(form, a.astype(jnp.float32), b.astype(jnp.float32))]
    pallas_call x0 -> x1, Pallas kernels: none -> 56.2 us  [attention(): pl.pallas_call(functools.partial(kernel, group), out_shape=jax.ShapeDtype...]
    slice x1 -> x0, other arithmetic: 11.4 us -> none  [together(): seen, total, high = (parts[..., :-2], parts[..., -2:-1], parts[..., -1:])]
    unnamed x4 -> x3, local copies, waits for them, and re-layouts: 11 us -> 1.74 us
    reduce_sum x3 -> x0, other arithmetic: 9.04 us -> none  [the longest x1 4.51 us: together(): jnp.sum(seen * scale, 0) / jnp.sum(total * scale, 0)]
    broadcast_in_dim x2 -> x0, local copies, waits for them, and re-layouts: 3.33 us -> none  [the longest x1 1.66 us: part_of(): jnp.sum(weights, -1, keepdims=True)]
  transfers between devices with their start and end apart: 1 -> 0, of which waited for: 1 -> 0; matrix products, arithmetic and copies ran while one was open for 0% -> 0% of each run, Pallas kernels for 0% -> 0%
where the time goes in v1:
time: 58.1 us; the launch traced here: 57.9 us
  Pallas kernels  56.2 us (97%)
  local copies, waits for them, and re-layouts  1.74 us (3%)
    pallas_call x1, Pallas kernels, attention(): pl.pallas_call(functools.partial(kernel, group), out_shape=jax.ShapeDtype...  56.2 us
    unnamed x3, local copies, waits for them, and re-layouts  1.74 us

profile of v1, /device:TPU:0, one launch (start us, length us, event | category | flops | bytes accessed | tf_op | source)
XLA Modules:
  0.0 57.9 jit_solution(5650732971332099752)
XLA Ops:
  0.0 0.0 copy-start
  0.0 1.0 %copy-done = bf16[32,48,128]{2,1,0:T(8,128)(2,1)S(1)} copy-done((bf16[32,48,128]{2,1,0:T(8,128)(2,1)S(1)}, bf16[32,48,128]{2,1,0:T(8,128)(2,1)}, u32[]{:S(2)}) %copy-start) | copy-done | bytes 393240
  1.0 56.2 %shard_map.37 = bf16[32,48,128]{2,1,0:T(8,128)(2,1)S(1)} custom-call(bf16[32,48,128]{2,1,0:T(8,128)(2,1)S(1)} %copy-done, bf16[32,8192,128]{2,1,0:T(8,128)(2,1)} %bitcast.k_hbm, bf16[32,8192,128]{2,1,0:T(8,128)(2,1)} %bitcast.1.v_hbm), custom_call_target="tpu_custom_call" | custom-call | flops 12884901888 | bytes 134217728 | tf_op jit(solution)/shard_map/pallas_call | solution.py:228
  57.2 0.7 %copy.5 = bf16[32,48,128]{2,1,0:T(8,128)(2,1)} copy(bf16[32,48,128]{2,1,0:T(8,128)(2,1)S(1)} %shard_map.37) | data formatting | bytes 786432
Async XLA Ops:
  0.0 1.0 %copy-start = (bf16[32,48,128]{2,1,0:T(8,128)(2,1)S(1)}, bf16[32,48,128]{2,1,0:T(8,128)(2,1)}, u32[]{:S(2)}) copy-start(bf16[32,48,128]{2,1,0:T(8,128)(2,1)} %q_ref.1) | copy-start | bytes 1179652

commit v2 on v1

v2 whole, which is shorter than its diff:
```python
import functools
import math

import jax
import jax.numpy as jnp
from jax import lax
from jax.experimental import pallas as pl
from jax.experimental.pallas import tpu as pltpu
from jax.sharding import PartitionSpec as P

F32, BF16 = jnp.float32, jnp.bfloat16
RING = 6
LAG = 4
DIRECT = 1
UNROLL = 2
TILE = 256
PIECES = 4
MESH = pl.DeviceIdType.MESH


def kernel(group, q_hbm, k_hbm, v_hbm, res, qbuf, kbuf, vbuf, s0, s1, m0, m1, p0, p1, parts, stats, ksem, vsem, qsem, lsem,
           po_send, ps_send, po_recv, ps_recv, r_send, r_recv):
    n, rows, d = k_hbm.shape
    heads = qbuf.shape[1]
    kv_heads = 8
    half = rows // 2
    tiles = half // TILE
    c = d**-0.5 * math.log2(math.e)
    me = lax.axis_index("sp")
    owned = n - DIRECT
    full = owned // group
    tail = full * group
    last = n - 1
    piece = half // PIECES

    def kcopy(i):
        return pltpu.make_async_copy(k_hbm.at[i], kbuf.at[lax.rem(i, RING)], ksem.at[lax.rem(i, RING)])

    def qcopy(i):
        return pltpu.make_async_copy(q_hbm.at[i], qbuf.at[lax.rem(i, RING)], qsem.at[lax.rem(i, RING)])

    def vcopy(i):
        return pltpu.make_async_copy(v_hbm.at[i], vbuf.at[lax.rem(i, RING)], vsem.at[lax.rem(i, RING)])

    def last_copies(k):
        out = []
        for h in range(2):
            at = pl.ds(h * half + k * piece, piece)
            out.append(pltpu.make_async_copy(v_hbm.at[last, at], vbuf.at[last % RING, at], lsem.at[2 * k + h]))
        return out

    for i in range(RING):
        qcopy(i).start()
        kcopy(i).start()
        if i:
            vcopy(i - 1).start()
    vcopy(RING - 1).start()

    barrier = pltpu.get_barrier_semaphore()
    for step in range(1, group):
        pl.semaphore_signal(barrier, inc=1, device_id={"sp": lax.rem(me + step, group)}, device_id_type=MESH)

    shape = (heads, TILE)
    own_head = lax.broadcasted_iota(jnp.int32, shape, 0) // (heads // kv_heads) == lax.broadcasted_iota(jnp.int32, shape, 1) % kv_heads
    mask = jnp.concatenate([own_head, own_head], 0)
    row = lax.broadcasted_iota(jnp.int32, (heads, d), 0)
    lane = lax.broadcasted_iota(jnp.int32, (heads, d), 1)

    def side(ref, slot, t):
        return jnp.concatenate([ref[slot, t * TILE : (t + 1) * TILE, :], ref[slot, half + t * TILE : half + (t + 1) * TILE, :]], 1)

    def scores(i, s_ref, m_ref):
        slot = lax.rem(i, RING)
        q = qbuf[slot]
        z = jnp.zeros_like(q)
        qq = jnp.concatenate([jnp.concatenate([q, z], 1), jnp.concatenate([z, q], 1)], 0)
        m = jnp.full((2 * heads, d), -jnp.inf, F32)
        for t in range(tiles):
            s = lax.dot_general(qq, side(kbuf, slot, t), (((1,), (1,)), ((), ())), preferred_element_type=F32)
            s = jnp.where(mask, s, -jnp.inf)
            s_ref[:, t * TILE : (t + 1) * TILE] = s
            m = jnp.maximum(m, jnp.maximum(s[:, :d], s[:, d:]))
        m_ref[...] = m

    def weights(i, s_ref, m_ref):
        m = m_ref[...]
        m = jnp.max(jnp.maximum(m[:heads], m[heads:]), 1, keepdims=True)
        m2 = jnp.concatenate([m, m], 0)
        l = jnp.zeros((2 * heads, d), F32)
        for t in range(tiles):
            p = jnp.exp2((s_ref[:, t * TILE : (t + 1) * TILE] - m2) * c)
            l = l + (p[:, :d] + p[:, d:])
            yield t, p.astype(BF16)
        l = jnp.sum(l[:heads] + l[heads:], 1, keepdims=True)
        stats[i, me] = jnp.sum(jnp.where(lane == row, m, jnp.where(lane == row + d // 2, l, 0.0)), 0, keepdims=True)

    def values(i, o, t, p):
        return o + lax.dot_general(p, side(vbuf, lax.rem(i, RING), t), (((1,), (0,)), ((), ())), preferred_element_type=F32)

    def keep(i, o):
        parts[i, me] = (o[:heads, :d] + o[heads:, d:]).astype(BF16)

    def attend(i, s_ref, m_ref):
        o = jnp.zeros((2 * heads, TILE), F32)
        for t, p in weights(i, s_ref, m_ref):
            o = values(i, o, t, p)
        keep(i, o)

    def store_weights(i, s_ref, m_ref, p_ref):
        for t, p in weights(i, s_ref, m_ref):
            p_ref[:, t * TILE : (t + 1) * TILE] = p

    def owner(i):
        return lax.rem(4 * n + owned + 2 - i, group)

    def index(i):
        if isinstance(i, int):
            return i // group if i < tail else full + i - tail
        return jnp.where(i < tail, i // group, full + i - tail)

    def part_copies(i, to):
        at = index(i)
        return [
            pltpu.make_async_remote_copy(ref.at[i, me], ref.at[i, me], send.at[at], recv.at[at], device_id={"sp": to}, device_id_type=MESH)
            for ref, send, recv in ((parts, po_send, po_recv), (stats, ps_send, ps_recv))
        ]

    def result_copy(i, to):
        return pltpu.make_async_remote_copy(res.at[i], res.at[i], r_send.at[index(i)], r_recv.at[index(i)], device_id={"sp": to}, device_id_type=MESH)

    def wait(ref, sem):
        pltpu.make_async_copy(ref, ref, sem).wait()

    def send_part(i):
        @pl.when(me != owner(i))
        def _():
            for copy in part_copies(i, owner(i)):
                copy.start()

    def send_direct(i):
        for step in range(group - 1, 0, -1):
            for copy in part_copies(i, lax.rem(me + step, group)):
                copy.start()

    def wait_parts(i):
        wait(parts.at[i, : group - 1], po_recv.at[index(i)])
        wait(stats.at[i, : group - 1], ps_recv.at[index(i)])

    def together(i):
        st = stats[i, :, 0, :]
        w = jnp.exp2((st - jnp.max(st, 0, keepdims=True)) * c)
        w = w / jnp.sum(w * pltpu.roll(st, d // 2, 1), 0, keepdims=True)
        w = jnp.transpose(w)
        out = w[:heads, :1] * parts[i, 0].astype(F32)
        for s in range(1, group):
            out = out + w[:heads, s : s + 1] * parts[i, s].astype(F32)
        res[i] = out.astype(BF16)

    def owner_step(i):
        @pl.when(me == owner(i))
        def _():
            wait_parts(i)
            together(i)
            for step in range(1, group):
                result_copy(i, lax.rem(me + step, group)).start()

    buffers = ((s0, m0), (s1, m1))

    def stretch(i, count):
        for h in range(count):
            qcopy(i + 1 + h).wait()
            kcopy(i + 1 + h).wait()
            vcopy(i + h).wait()
        for h in range(count):
            scores(i + 1 + h, *buffers[(h + 1) % 2])
            attend(i + h, *buffers[h % 2])
        if not isinstance(i, int):
            for h in range(count):
                @pl.when(i + h + 1 + RING < n)
                def _():
                    qcopy(i + h + 1 + RING).start()
                    kcopy(i + h + 1 + RING).start()

                @pl.when(i + h + RING < last)
                def _():
                    vcopy(i + h + RING).start()

                @pl.when(i + h + RING == last)
                def _():
                    for k in range(PIECES):
                        for copy in last_copies(k):
                            copy.start()
        for h in range(count):
            send_part(i + h)
        for h in range(count):
            if isinstance(i, int):
                owner_step(i + h - LAG)
            else:
                pl.when(i + h >= LAG)(lambda: owner_step(i + h - LAG))

    qcopy(0).wait()
    kcopy(0).wait()
    scores(0, s0, m0)
    qcopy(RING).start()
    kcopy(RING).start()
    pl.semaphore_wait(barrier, group - 1)

    def body(j, _):
        stretch(UNROLL * j, UNROLL)
        return 0

    lax.fori_loop(0, (n - 4) // UNROLL, body, 0)
    stretch(n - 4, 2)

    qcopy(last).wait()
    kcopy(last).wait()
    scores(last, s1, m1)
    store_weights(last - 1, s0, m0, p0)
    owner_step(last - 1 - LAG)
    vcopy(last - 1).wait()
    store_weights(last, s1, m1, p1)
    o = jnp.zeros((2 * heads, TILE), F32)
    for t in range(tiles):
        o = values(last - 1, o, t, p0[:, t * TILE : (t + 1) * TILE])
    keep(last - 1, o)
    if last - 1 < owned:
        send_part(last - 1)
    else:
        send_direct(last - 1)
    o = jnp.zeros((2 * heads, TILE), F32)
    for t in range(tiles):
        if t % (tiles // PIECES) == 0:
            for copy in last_copies(t // (tiles // PIECES)):
                copy.wait()
        o = values(last, o, t, p1[:, t * TILE : (t + 1) * TILE])
    keep(last, o)
    send_direct(last)
    for i in range(last - LAG, owned):
        owner_step(i)
    for i in range(owned, n):
        wait_parts(i)
        together(i)

    for b in range(full):
        wait(parts.at[0, : group - 1], po_send.at[b])
        wait(stats.at[0, : group - 1], ps_send.at[b])
        wait(res.at[: group - 1], r_send.at[b])
        wait(res.at[: group - 1], r_recv.at[b])
    for i in range(tail, owned):
        @pl.when(me != owner(i))
        def _():
            wait(res.at[i], r_recv.at[index(i)])
            wait(parts.at[i, 0], po_send.at[index(i)])
            wait(stats.at[i, 0], ps_send.at[index(i)])

        @pl.when(me == owner(i))
        def _():
            wait(res.at[: group - 1], r_send.at[index(i)])
    for i in range(owned, n):
        wait(parts.at[i, : group - 1], po_send.at[index(i)])
        wait(stats.at[i, : group - 1], ps_send.at[index(i)])


def attention(group, q, k, v):
    n, heads, d = q.shape
    rows = k.shape[1] * k.shape[2]
    q = pltpu.with_memory_space_constraint(q, pltpu.HBM)
    k, v = k.reshape(n, rows, d), v.reshape(n, rows, d)
    full = (n - DIRECT) // group
    sems = full + n - full * group
    hbm = pl.BlockSpec(memory_space=pltpu.HBM)
    return pl.pallas_call(
        functools.partial(kernel, group),
        out_shape=jax.ShapeDtypeStruct((n, heads, d), BF16),
        in_specs=[hbm, hbm, hbm],
        out_specs=pl.BlockSpec(memory_space=pltpu.VMEM),
        scratch_shapes=[
            pltpu.VMEM((RING, heads, d), BF16),
            pltpu.VMEM((RING, rows, d), BF16),
            pltpu.VMEM((RING, rows, d), BF16),
            pltpu.VMEM((2 * heads, rows // 2), F32),
            pltpu.VMEM((2 * heads, rows // 2), F32),
            pltpu.VMEM((2 * heads, d), F32),
            pltpu.VMEM((2 * heads, d), F32),
            pltpu.VMEM((2 * heads, rows // 2), BF16),
            pltpu.VMEM((2 * heads, rows // 2), BF16),
            pltpu.VMEM((n, group, heads, d), BF16),
            pltpu.VMEM((n, group, 1, d), F32),
            pltpu.SemaphoreType.DMA((RING,)),
            pltpu.SemaphoreType.DMA((RING,)),
            pltpu.SemaphoreType.DMA((RING,)),
            pltpu.SemaphoreType.DMA((2 * PIECES,)),
        ]
        + [pltpu.SemaphoreType.DMA((sems,))] * 6,
        compiler_params=pltpu.CompilerParams(collective_id=0, has_side_effects=True, vmem_limit_bytes=46 * 2**20),
        cost_estimate=pl.CostEstimate(flops=8 * n * heads * rows * d, bytes_accessed=4 * n * rows * d, transcendentals=n * heads * rows),
    )(q, k, v)


def solution(mesh):
    cache = P("dp", "sp", None, None)
    return jax.shard_map(
        functools.partial(attention, mesh.shape["sp"]),
        mesh=mesh,
        in_specs=(P("dp", None, None), cache, cache),
        out_specs=P("dp", None, None),
        check_vma=False,
    )
```

time: 58.1 us -> 54.1 us (0.931)
  Pallas kernels: 56.2 us -> 53.1 us
  local copies, waits for them, and re-layouts: 1.74 us -> 0.75 us
    pallas_call x1, Pallas kernels: 56.2 us -> 53.1 us  [attention(): pl.pallas_call(functools.partial(kernel, group), out_shape=jax.ShapeDtype...]
    unnamed x3 -> x1, local copies, waits for them, and re-layouts: 1.74 us -> 0.75 us
where the time goes in v2:
time: 54.1 us; the launch traced here: 53.9 us
  Pallas kernels  53.1 us (98%)
  local copies, waits for them, and re-layouts  0.75 us (1%)
    pallas_call x1, Pallas kernels, attention(): pl.pallas_call(functools.partial(kernel, group), out_shape=jax.ShapeDtype...  53.1 us

profile of v2, /device:TPU:0, one launch (start us, length us, event | category | flops | bytes accessed | tf_op | source)
XLA Modules:
  0.0 53.9 jit_solution(12663265635269383270)
XLA Ops:
  0.0 53.1 %shard_map.37 = bf16[32,48,128]{2,1,0:T(8,128)(2,1)S(1)} custom-call(bf16[32,48,128]{2,1,0:T(8,128)(2,1)} %q_hbm.1, bf16[32,8192,128]{2,1,0:T(8,128)(2,1)} %bitcast.k_hbm, bf16[32,8192,128]{2,1,0:T(8,128)(2,1)} %bitcast.1.v_hbm), custom_call_target="tpu_custom_call" | custom-call | flops 12884901888 | bytes 134217728 | tf_op jit(solution)/shard_map/pallas_call | solution.py:272
  53.1 0.7 %copy.5 = bf16[32,48,128]{2,1,0:T(8,128)(2,1)} copy(bf16[32,48,128]{2,1,0:T(8,128)(2,1)S(1)} %shard_map.37) | data formatting | bytes 786432

commit v3 on v2

--- a/solution.py
+++ b/solution.py
@@ -10,7 +10,8 @@
 
 F32, BF16 = jnp.float32, jnp.bfloat16
 RING = 6
-LAG = 4
+LAG = 6
+END_LAG = 4
 DIRECT = 1
 UNROLL = 2
 TILE = 256
@@ -192,11 +193,12 @@
                             copy.start()
         for h in range(count):
             send_part(i + h)
+        if isinstance(i, int):
+            for x in range(i - LAG, i + count - END_LAG):
+                owner_step(x)
+            return
         for h in range(count):
-            if isinstance(i, int):
-                owner_step(i + h - LAG)
-            else:
-                pl.when(i + h >= LAG)(lambda: owner_step(i + h - LAG))
+            pl.when(i + h >= LAG)(lambda: owner_step(i + h - LAG))
 
     qcopy(0).wait()
     kcopy(0).wait()
@@ -216,7 +218,7 @@
     kcopy(last).wait()
     scores(last, s1, m1)
     store_weights(last - 1, s0, m0, p0)
-    owner_step(last - 1 - LAG)
+    owner_step(last - 1 - END_LAG)
     vcopy(last - 1).wait()
     store_weights(last, s1, m1, p1)
     o = jnp.zeros((2 * heads, TILE), F32)
@@ -235,7 +237,7 @@
         o = values(last, o, t, p1[:, t * TILE : (t + 1) * TILE])
     keep(last, o)
     send_direct(last)
-    for i in range(last - LAG, owned):
+    for i in range(last - END_LAG, owned):
         owner_step(i)
     for i in range(owned, n):
         wait_parts(i)

time: 54.1 us -> 54.2 us (level)
  no operation moved by 1% of the time
where the time goes in v3:
time: 54.2 us; the launch traced here: 54 us
  Pallas kernels  53.2 us (98%)
  local copies, waits for them, and re-layouts  0.75 us (1%)
    pallas_call x1, Pallas kernels, attention(): pl.pallas_call(functools.partial(kernel, group), out_shape=jax.ShapeDtype...  53.2 us

profile of v3, /device:TPU:0, one launch (start us, length us, event | category | flops | bytes accessed | tf_op | source)
XLA Modules:
  0.0 54.0 jit_solution(457848594090343150)
XLA Ops:
  0.0 53.2 %shard_map.37 = bf16[32,48,128]{2,1,0:T(8,128)(2,1)S(1)} custom-call(bf16[32,48,128]{2,1,0:T(8,128)(2,1)} %q_hbm.1, bf16[32,8192,128]{2,1,0:T(8,128)(2,1)} %bitcast.k_hbm, bf16[32,8192,128]{2,1,0:T(8,128)(2,1)} %bitcast.1.v_hbm), custom_call_target="tpu_custom_call" | custom-call | flops 12884901888 | bytes 134217728 | tf_op jit(solution)/shard_map/pallas_call | solution.py:274
  53.2 0.7 %copy.5 = bf16[32,48,128]{2,1,0:T(8,128)(2,1)} copy(bf16[32,48,128]{2,1,0:T(8,128)(2,1)S(1)} %shard_map.37) | data formatting | bytes 786432
